TPU v7x, 32 devices: a whole 2x2x4 slice. The times are simulated.
32 devices in a mesh: ga: 2 (over y), gx: 4 (over z), gy: 2 (over x), col: 2 (over core).
Axes of the slice: x: 2, y: 2, z: 4, core: 2. Of those that a mesh axis runs over, the one named last changes fastest.
Arguments:
- pair_rep: bfloat16 [2, 160, 160, 128], P('ga', 'gx', 'gy'), parts along dimension 0, may hold values from -6 to 6
- pair_mask: int32 [2, 160, 160], P('ga', 'gx', 'gy'), parts along dimension 0, may hold values 0 or 1
- amax_history: float32 [2, 128], P(None, 'col'), may hold values from 0.3 to 3
- in_gain: float32 [128], replicated, may hold values from 0.5 to 1.5
- in_bias: float32 [128], replicated, may hold values from -3 to 3
- proj_weight: bfloat16 [128, 4, 128], P(None, None, 'col'), may hold values from -0.5 to 0.5
- gate_weight: bfloat16 [128, 128], P(None, 'col'), may hold values from -0.5 to 0.5
- out_gain: float32 [128], replicated, may hold values from 0.5 to 1.5
- out_bias: float32 [128], replicated, may hold values from -3 to 3
- out_weight: bfloat16 [128, 128], P(None, 'col'), may hold values from -0.5 to 0.5
Outputs:
- update: bfloat16 [2, 160, 160, 128], P('ga', 'gx', 'gy', 'col'), parts along dimension 0
- new_amax: float32 [4, 128], P('ga', 'col'), parts along dimension 0
There are 2 independent parts, one for each index of `ga`. A program takes and returns all parts, laid end to end along the dimension named above; an argument that names none is the same for every part. Nothing has to cross between parts.
All inputs are finite; a program needn't handle non-finite values. No bound on the sum of `pair_mask` on one device may be relied on, other than what follows from the above.
Results may differ from a plain program's by a relative error of at most 0.0065.
Values may be sent and summed in bfloat16 or wider, within the bound.
A program may use at most 128 MiB of HBM per device.

v0:
```python
import jax
import jax.numpy as jnp
from jax import lax
from jax.sharding import PartitionSpec as P

epsilon = 1e-05
format_limit = 448.0


def broadcast(block, axis, holder):
    block = jnp.where(lax.axis_index(axis) == holder, block, jnp.zeros_like(block))
    return lax.psum(block, axis)


def layer_norm(values, gain, bias):
    average = jnp.mean(values, axis=-1, keepdims=True)
    spread = jnp.mean(jnp.square(values - average), axis=-1, keepdims=True)
    return (values - average) * lax.rsqrt(spread + epsilon) * gain + bias


def crop_triangle(left_q, right_q):
    wide_rows = lax.all_gather(right_q, "gy", axis=2, tiled=True)
    row_ratio = lax.axis_size("gx") // lax.axis_size("gy")
    first_root = lax.axis_index("gy") * row_ratio
    received = [
        broadcast(wide_rows, "gx", first_root + offset_step) for offset_step in range(row_ratio)
    ]
    panel = jnp.concatenate(received, axis=1)
    return jnp.einsum(
        "cik,cjk->cij",
        lax.all_gather(left_q, "gy", axis=2, tiled=True),
        panel,
        preferred_element_type=jnp.float32,
    )


def on_device(
    pair_rep,
    pair_mask,
    amax_history,
    in_gain,
    in_bias,
    proj_weight,
    gate_weight,
    out_gain,
    out_bias,
    out_weight,
):
    normed = layer_norm(pair_rep.astype(jnp.float32), in_gain, in_bias).astype(jnp.bfloat16)
    projected = jnp.einsum(
        "bikd,dsc->scbik", normed, proj_weight, preferred_element_type=jnp.float32
    )
    masking = pair_mask.astype(jnp.float32)[None]
    left_proj = masking * jax.nn.sigmoid(projected[1]) * projected[0]
    right_proj = masking * jax.nn.sigmoid(projected[3]) * projected[2]
    local_max = jnp.stack(
        [jnp.max(jnp.abs(left_proj), axis=(1, 2, 3)), jnp.max(jnp.abs(right_proj), axis=(1, 2, 3))]
    )
    new_amax = lax.pmax(local_max, ("gx", "gy"))
    scales = amax_history / format_limit
    left_q = jnp.clip(
        left_proj / scales[0][:, None, None, None], -format_limit, format_limit
    ).astype(jnp.bfloat16)
    right_q = jnp.clip(
        right_proj / scales[1][:, None, None, None], -format_limit, format_limit
    ).astype(jnp.bfloat16)
    products = jnp.stack([crop_triangle(left_q[:, 0], right_q[:, 0])], axis=1)
    triangle = (products * (scales[0] * scales[1])[:, None, None, None]).astype(jnp.bfloat16)
    gathered = lax.all_gather(triangle, "col", axis=0, tiled=True).astype(jnp.float32)
    average = jnp.mean(gathered, axis=0, keepdims=True)
    spread = jnp.mean(jnp.square(gathered - average), axis=0, keepdims=True)
    tnorm = (
        (gathered - average) * lax.rsqrt(spread + epsilon) * out_gain[:, None, None, None]
        + out_bias[:, None, None, None]
    ).astype(jnp.bfloat16)
    mixing = jnp.einsum("cbij,cd->bijd", tnorm, out_weight, preferred_element_type=jnp.float32)
    gating = jax.nn.sigmoid(
        jnp.einsum("bijd,dc->bijc", normed, gate_weight, preferred_element_type=jnp.float32)
    )
    update = (gating * mixing).astype(jnp.bfloat16)
    return (update, new_amax)


def solution(mesh):
    placed = (
        P("ga", "gx", "gy", None),
        P("ga", "gx", "gy"),
        P(None, "col"),
        P(),
        P(),
        P(None, None, "col"),
        P(None, "col"),
        P(),
        P(),
        P(None, "col"),
    )
    return jax.shard_map(
        on_device,
        mesh=mesh,
        in_specs=placed,
        out_specs=(P("ga", "gx", "gy", "col"), P("ga", "col")),
        check_vma=False,
    )
```

profile of v0, /device:TPU:0, one launch (start us, length us, event | category | flops | bytes accessed | tf_op | source)
XLA Modules:
  0.0 166.5 jit_solution(14759591514947378513)
XLA Ops:
  7.2 0.0 copy-start
  7.2 0.0 copy-start.2
  7.2 0.0 copy-start.6
  7.2 0.0 copy-start.7
  7.2 0.0 all-reduce.3.cloned.1.call-start
  7.3 0.8 broadcast_multiply_fusion.2
  8.0 0.7 convert_bitcast_fusion.1
  8.8 1.6 convert_reduce_fusion.1
  10.3 0.0 copy-done.2
  10.4 1.2 fusion.13
  11.6 0.0 copy-done
  11.6 0.0 copy-done.6
  11.6 0.0 copy-done.7
  11.6 2.1 %convolution_bitcast_fusion = f32[4,64,40,80]{3,1,0,2:T(8,128)S(1)} fusion(bf16[1,40,80,128]{3,2,1,0:T(8,128)(2,1)S(1)} %copy-done.2, f32[128]{0:T(128)S(1)} %copy-done.6, f32[128]{0:T(128)S(1)} %copy-done.7, f32[40,80]{1,0:T(8,128)S(1)} %add_rsqrt_fusion.1, f32[40,80]{1,0:T(8,128)S(1)} %broadcast_multiply_fusion.1, bf16[128,4,64]{0,2,1:T(8,128)(2,1)S(1)} %copy-done), kind=kOutput, calls=%fused_computation.13 | convolution fusion | flops 212172800 | bytes 4188160 | tf_op jit(solution)/shard_map/bikd,dsc->scbik/dot_general | solution.py:50
  13.7 0.0 copy-start.1
  13.7 2.3 %fusion.45 = (bf16[64,40,80]{2,0,1:T(8,128)(2,1)S(1)}, bf16[64,40,80]{2,0,1:T(8,128)(2,1)}) fusion(f32[4,64,40,80]{3,1,0,2:T(8,128)S(1)} %convolution_bitcast_fusion, f32[64]{0:T(128)S(1)} %get-tuple-element.10, f32[40,80]{1,0:T(8,128)S(1)} %convert_bitcast_fusion.1, f32[64]{0:T(128)S(1)} %get-tuple-element.11), kind=kLoop, calls=%fused_computation.56 | loop fusion | flops 3276800 | bytes 4109312 | tf_op jit(solution)/shard_map/convert_element_type | solution.py:66
  16.0 0.2 copy-done.1
  16.3 0.5 copy.22
  16.7 21.9 %all_gather.10 = bf16[64,40,160]{0,1,2:T(8,128)(2,1)S(1)} all-gather(bf16[64,40,80]{0,1,2:T(8,128)(2,1)S(1)} %copy.22), channel_id=1, replica_groups=mesh['ga'=2,'gx'=4,'gy'=2,'col'=2] {'gy'}, dimensions={2}, use_global_device_ids=true | all-gather | bytes 1228800 | tf_op jit(solution)/shard_map/all_gather | solution.py:22
  38.6 4.0 %copy.23 = bf16[64,40,160]{2,1,0:T(8,128)(2,1)} copy(bf16[64,40,160]{0,1,2:T(8,128)(2,1)S(1)} %all_gather.10) | data formatting | bytes 1638400 | tf_op jit(solution)/shard_map/all_gather | solution.py:22
  42.6 3.0 %broadcast_select_fusion.1 = (bf16[64,40,160]{2,1,0:T(8,128)(2,1)}, bf16[64,40,160]{2,1,0:T(8,128)(2,1)}) fusion(bf16[64,40,160]{2,1,0:T(8,128)(2,1)} %copy.23, pred[]{:T(512)S(6)} %eq.6, pred[]{:T(512)S(6)} %eq.7), kind=kLoop, calls=%fused_computation.61 | loop fusion | flops 819200 | bytes 2457602 | tf_op jit(solution)/shard_map/jit(_where)/select_n | solution.py:11
  45.7 0.0 copy-start.3
  45.7 0.0 all-reduce.3.cloned.1.call-update
  45.7 1.1 copy-done.3
  46.8 0.5 copy.20
  47.2 20.1 %all_gather.9 = bf16[64,40,160]{0,1,2:T(8,128)(2,1)S(1)} all-gather(bf16[64,40,80]{0,1,2:T(8,128)(2,1)S(1)} %copy.20), channel_id=1, replica_groups=mesh['ga'=2,'gx'=4,'gy'=2,'col'=2] {'gy'}, dimensions={2}, use_global_device_ids=true | all-gather | bytes 1228800 | tf_op jit(solution)/shard_map/all_gather | solution.py:31
  67.3 4.0 %copy.25 = bf16[64,40,160]{2,1,0:T(8,128)(2,1)} copy(bf16[64,40,160]{0,1,2:T(8,128)(2,1)S(1)} %all_gather.9) | data formatting | bytes 1638400 | tf_op jit(solution)/shard_map/all_gather | solution.py:31
  71.4 3.5 %fusion.37 = (f32[64]{0:T(128)S(1)}, f32[64]{0:T(128)S(1)}) fusion(f32[4,64,40,80]{3,1,0,2:T(8,128)} %copy-done.1, f32[40,80]{1,0:T(8,128)S(1)} %convert_bitcast_fusion.1), kind=kLoop, calls=%fused_computation.43 | loop fusion | flops 2867072 | bytes 3290112 | tf_op jit(solution)/shard_map/reduce_max | solution.py:57
  74.9 23.4 %pmax.7 = f32[2,64]{1,0:T(2,128)} all-reduce(f32[2,64]{1,0:T(2,128)S(1)} %pad_maximum_fusion), channel_id=1, replica_groups=mesh['ga'=2,'gx'=4,'gy'=2,'col'=2] {'gx','gy'}, use_global_device_ids=true, to_apply=%region_8.9 | all-reduce | flops 128 | bytes 1024 | tf_op jit(solution)/shard_map/pmax | solution.py:59
  98.2 0.5 fusion.58
  98.7 0.0 copy-start.4
  98.7 2.0 %fusion.22 = f32[40,80,64]{1,2,0:T(8,128)S(1)} fusion(bf16[1,40,80,128]{3,2,1,0:T(8,128)(2,1)S(1)} %copy-done.2, f32[128]{0:T(128)S(1)} %copy-done.6, f32[128]{0:T(128)S(1)} %copy-done.7, f32[40,80]{1,0:T(8,128)S(1)} %add_rsqrt_fusion.1, f32[40,80]{1,0:T(8,128)S(1)} %broadcast_multiply_fusion.1, bf16[128,64]{0,1:T(8,128)(2,1)} %param.16), kind=kOutput, calls=%fused_computation.27 | convolution fusion | flops 55500800 | bytes 1681408 | tf_op jit(solution)/shard_map/bijd,dc->bijc/dot_general | solution.py:78
  100.7 51.0 %all-reduce.3.cloned.1.call-done = (bf16[64,40,160]{2,1,0:T(8,128)(2,1)}, bf16[64,40,160]{2,1,0:T(8,128)(2,1)}) async-done(((bf16[64,40,160]{2,1,0:T(8,128)(2,1)}, bf16[64,40,160]{2,1,0:T(8,128)(2,1)}), (bf16[64,40,160]{2,1,0:T(8,128)(2,1)}, bf16[64,40,160]{2,1,0:T(8,128)(2,1)})) %all-reduce.3.cloned.1.call-update) | async-done | bytes 1638416 | tf_op jit(solution)/shard_map/psum | solution.py:12
  151.7 0.0 copy-done.4
  151.7 2.5 %fusion.24 = bf16[64,40,80]{2,1,0:T(8,128)(2,1)S(1)} fusion(bf16[64,40,160]{2,1,0:T(8,128)(2,1)S(1)} %copy-done.4, bf16[64,40,160]{2,1,0:T(8,128)(2,1)} %get-tuple-element.4, bf16[64,40,160]{2,1,0:T(8,128)(2,1)} %get-tuple-element.5, f32[64]{0:T(128)} %fusion.58), kind=kOutput, calls=%fused_computation.29 | convolution fusion | flops 69222400 | bytes 2867456 | tf_op jit(solution)/shard_map/cik,cjk->cij/dot_general | solution.py:29
  154.2 2.7 %all-gather = bf16[128,40,80]{2,1,0:T(8,128)(2,1)S(1)} all-gather(bf16[64,40,80]{2,1,0:T(8,128)(2,1)S(1)} %fusion.24), channel_id=2, replica_groups=mesh['ga'=2,'gx'=4,'gy'=2,'col'=2] {'col'}, dimensions={0}, use_global_device_ids=true | all-gather | bytes 1228800 | tf_op jit(solution)/shard_map/all_gather | solution.py:69
  157.0 0.0 copy-start.8
  157.0 0.0 copy-start.9
  157.0 0.3 convert_reduce_fusion
  157.3 0.5 fusion.3
  157.8 0.0 copy-done.8
  157.8 0.0 copy-done.9
  157.8 0.0 copy-start.5
  157.8 0.5 fusion.27
  158.4 0.2 copy-done.5
  158.5 1.2 fusion.47
  (6 shorter events, 0.0 us)
Async XLA Ops:
  7.2 4.4 %copy-start = (bf16[128,4,64]{0,2,1:T(8,128)(2,1)S(1)}, bf16[128,4,64]{0,2,1:T(8,128)(2,1)}, u32[]{:S(2)}) copy-start(bf16[128,4,64]{0,2,1:T(8,128)(2,1)} %param.15) | copy-start | bytes 196612
  7.2 3.2 %copy-start.2 = (bf16[1,40,80,128]{3,2,1,0:T(8,128)(2,1)S(1)}, bf16[1,40,80,128]{3,2,1,0:T(8,128)(2,1)}, u32[]{:S(2)}) copy-start(bf16[1,40,80,128]{3,2,1,0:T(8,128)(2,1)} %param.10) | copy-start | bytes 2457604
  7.2 4.4 %copy-start.6 = (f32[128]{0:T(128)S(1)}, f32[128]{0:T(128)}, u32[]{:S(2)}) copy-start(f32[128]{0:T(128)} %param.14) | copy-start | bytes 1540
  7.2 4.4 %copy-start.7 = (f32[128]{0:T(128)S(1)}, f32[128]{0:T(128)}, u32[]{:S(2)}) copy-start(f32[128]{0:T(128)} %param.13) | copy-start | bytes 1540
  7.2 144.5 %all-reduce.3.cloned.1.call-start = ((), (), s32[]{:S(2)}) async-start(), calls=%async_computation | async-start | bytes 5242880 | tf_op jit(solution)/shard_map/psum | solution.py:12
  13.7 2.5 %copy-start.1 = (f32[4,64,40,80]{3,1,0,2:T(8,128)}, f32[4,64,40,80]{3,1,0,2:T(8,128)S(1)}, u32[]{:S(2)}) copy-start(f32[4,64,40,80]{3,1,0,2:T(8,128)S(1)} %convolution_bitcast_fusion) | copy-start | bytes 9830404
  45.7 1.1 copy-start.3
  98.7 53.0 %copy-start.4 = (bf16[64,40,160]{2,1,0:T(8,128)(2,1)S(1)}, bf16[64,40,160]{2,1,0:T(8,128)(2,1)}, u32[]{:S(2)}) copy-start(bf16[64,40,160]{2,1,0:T(8,128)(2,1)} %copy.25) | copy-start | bytes 2457604
  157.0 0.8 copy-start.8
  157.0 0.8 copy-start.9
  157.8 0.7 copy-start.5
Sparse Core Ops, SparseCore 0:
  45.8 105.8 all-reduce.2
where the time goes:
time: 167 us
  blocking collectives  68.1 us (41%)
  waiting for transfers between devices  51 us (31%)
  other arithmetic  14.9 us (9%)
  between operations  14.2 us (9%)
  local copies, waits for them, and re-layouts  10.5 us (6%)
  matrix products  7.79 us (5%)
    psum x1, waiting for transfers between devices, broadcast(): return lax.psum(block, axis)  51 us
    pmax x1, blocking collectives, on_device(): new_amax = lax.pmax(local_max, ('gx', 'gy'))  23.4 us
    all_gather x1, blocking collectives, crop_triangle(): wide_rows = lax.all_gather(right_q, 'gy', axis=2, tiled=True)  21.9 us
    all_gather x1, blocking collectives, crop_triangle(): lax.all_gather(left_q, 'gy', axis=2, tiled=True)  20.1 us
    all_gather x1, local copies, waits for them, and re-layouts, crop_triangle(): lax.all_gather(left_q, 'gy', axis=2, tiled=True)  4.05 us
    all_gather x1, local copies, waits for them, and re-layouts, crop_triangle(): wide_rows = lax.all_gather(right_q, 'gy', axis=2, tiled=True)  4.02 us
    reduce_max x1, other arithmetic, on_device(): jnp.max(jnp.abs(left_proj), axis=(1, 2, 3))  3.47 us
  transfers between devices with their start and end apart: 1, of which 1 were waited for; matrix products, arithmetic and copies ran while one was open for 6% of the time, Pallas kernels for 0%

commit v1 on v0

--- a/solution.py
+++ b/solution.py
@@ -7,9 +7,13 @@
 format_limit = 448.0
 
 
+def patches_divide(inner_x, shard_axis):
+    return lax.all_gather(inner_x, axis_name=shard_axis).sum(axis=0)
+
+
 def broadcast(block, axis, holder):
     block = jnp.where(lax.axis_index(axis) == holder, block, jnp.zeros_like(block))
-    return lax.psum(block, axis)
+    return patches_divide(block, axis)
 
 
 def layer_norm(values, gain, bias):

time: 167 us -> 264 us (1.58)
  waiting for transfers between devices: 51 us -> 134 us
  other arithmetic: 14.9 us -> 22.7 us
  local copies, waits for them, and re-layouts: 10.5 us -> 15.7 us
    all_gather x0 -> x2, waiting for transfers between devices: none -> 134 us  [patches_divide(): return lax.all_gather(inner_x, axis_name=shard_axis).sum(axis=0)]
    psum x1 -> x0, waiting for transfers between devices: 51 us -> none  [broadcast(): return lax.psum(block, axis)]
    reduce_sum x0 -> x2, other arithmetic: none -> 9.83 us  [patches_divide(): return lax.all_gather(inner_x, axis_name=shard_axis).sum(axis=0)]
    select_n x0 -> x2, local copies, waits for them, and re-layouts: none -> 9.29 us  [broadcast(): jnp.where(lax.axis_index(axis) == holder, block, jnp.zeros_like(block))]
    all_gather x1 -> x0, local copies, waits for them, and re-layouts: 4.02 us -> none  [crop_triangle(): wide_rows = lax.all_gather(right_q, 'gy', axis=2, tiled=True)]
  transfers between devices with their start and end apart: 1 -> 2, of which waited for: 1 -> 2; matrix products, arithmetic and copies ran while one was open for 6% -> 7% of each run, Pallas kernels for 0% -> 0%
where the time goes in v1:
time: 264 us; the launch traced here: 263 us
  waiting for transfers between devices  134 us (51%)
  blocking collectives  68.1 us (26%)
  other arithmetic  22.7 us (9%)
  local copies, waits for them, and re-layouts  15.7 us (6%)
  between operations  14.2 us (5%)
  matrix products  7.67 us (3%)
    all_gather x2, waiting for transfers between devices, patches_divide(): return lax.all_gather(inner_x, axis_name=shard_axis).sum(axis=0)  134 us
    pmax x1, blocking collectives, on_device(): new_amax = lax.pmax(local_max, ('gx', 'gy'))  23.4 us
    all_gather x1, blocking collectives, crop_triangle(): wide_rows = lax.all_gather(right_q, 'gy', axis=2, tiled=True)  21.9 us
    all_gather x1, blocking collectives, crop_triangle(): lax.all_gather(left_q, 'gy', axis=2, tiled=True)  20.1 us
    reduce_sum x2, other arithmetic, patches_divide(): return lax.all_gather(inner_x, axis_name=shard_axis).sum(axis=0)  9.83 us
    select_n x2, local copies, waits for them, and re-layouts, broadcast(): jnp.where(lax.axis_index(axis) == holder, block, jnp.zeros_like(block))  9.29 us
  transfers between devices with their start and end apart: 2, of which 2 were waited for; matrix products, arithmetic and copies ran while one was open for 7% of the time, Pallas kernels for 0%

profile of v1, /device:TPU:0, one launch (start us, length us, event | category | flops | bytes accessed | tf_op | source)
XLA Modules:
  0.0 263.0 jit_solution(6233949567339225766)
XLA Ops:
  7.2 0.0 copy-start
  7.2 0.0 copy-start.2
  7.2 0.0 copy-start.6
  7.2 0.0 copy-start.7
  7.2 0.0 all-gather.6.cloned.1.call-start
  7.3 0.8 broadcast_multiply_fusion.2
  8.0 0.7 convert_bitcast_fusion.1
  8.8 1.6 convert_reduce_fusion.1
  10.3 0.0 copy-done.2
  10.4 1.2 fusion.13
  11.6 0.0 copy-done
  11.6 0.0 copy-done.6
  11.6 0.0 copy-done.7
  11.6 2.1 convolution_bitcast_fusion
  13.7 0.0 copy-start.1
  13.7 2.4 fusion.45
  16.1 0.2 copy-done.1
  16.3 0.5 copy.45
  16.8 21.9 %all_gather.22 = bf16[64,40,160]{0,1,2:T(8,128)(2,1)S(1)} all-gather(bf16[64,40,80]{0,1,2:T(8,128)(2,1)S(1)} %copy.45), channel_id=1, replica_groups=mesh['ga'=2,'gx'=4,'gy'=2,'col'=2] {'gy'}, dimensions={2}, use_global_device_ids=true | all-gather | bytes 1228800 | tf_op jit(solution)/shard_map/all_gather | solution.py:26
  38.7 1.4 broadcast_select_fusion.1
  40.1 5.2 %copy.46 = bf16[64,40,160]{2,1,0:T(8,128)(2,1)} copy(bf16[64,40,160]{0,1,2:T(8,128)(2,1)} %get-tuple-element.6) | data formatting | bytes 1638400 | tf_op jit(solution)/shard_map/jit(_where)/select_n | solution.py:15
  45.3 0.0 all-gather.6.cloned.1.call-update
  45.3 0.0 all-gather.8.cloned.1.call-start
  45.4 4.1 %copy.48 = bf16[64,40,160]{2,1,0:T(8,128)(2,1)} copy(bf16[64,40,160]{0,1,2:T(8,128)(2,1)S(1)} %get-tuple-element.7) | data formatting | bytes 1638400 | tf_op jit(solution)/shard_map/jit(_where)/select_n | solution.py:15
  49.4 0.0 all-gather.8.cloned.1.call-update
  49.5 1.1 copy-done.3
  50.5 0.5 copy.43
  51.0 20.1 %all_gather.21 = bf16[64,40,160]{0,1,2:T(8,128)(2,1)S(1)} all-gather(bf16[64,40,80]{0,1,2:T(8,128)(2,1)S(1)} %copy.43), channel_id=1, replica_groups=mesh['ga'=2,'gx'=4,'gy'=2,'col'=2] {'gy'}, dimensions={2}, use_global_device_ids=true | all-gather | bytes 1228800 | tf_op jit(solution)/shard_map/all_gather | solution.py:35
  71.1 4.0 %copy.52 = bf16[64,40,160]{2,1,0:T(8,128)(2,1)} copy(bf16[64,40,160]{0,1,2:T(8,128)(2,1)S(1)} %all_gather.21) | data formatting | bytes 1638400 | tf_op jit(solution)/shard_map/all_gather | solution.py:35
  75.1 3.5 %fusion.37 = (f32[64]{0:T(128)S(1)}, f32[64]{0:T(128)S(1)}) fusion(f32[4,64,40,80]{3,1,0,2:T(8,128)} %copy-done.1, f32[40,80]{1,0:T(8,128)S(1)} %convert_bitcast_fusion.1), kind=kLoop, calls=%fused_computation.45 | loop fusion | flops 2867072 | bytes 3290112 | tf_op jit(solution)/shard_map/reduce_max | solution.py:61
  78.6 23.4 %pmax.7 = f32[2,64]{1,0:T(2,128)} all-reduce(f32[2,64]{1,0:T(2,128)S(1)} %pad_maximum_fusion), channel_id=1, replica_groups=mesh['ga'=2,'gx'=4,'gy'=2,'col'=2] {'gx','gy'}, use_global_device_ids=true, to_apply=%region_8.9 | all-reduce | flops 128 | bytes 1024 | tf_op jit(solution)/shard_map/pmax | solution.py:63
  102.0 0.0 copy-done.10
  102.0 1.9 fusion.22
  103.9 41.3 %all-gather.6.cloned.1.call-done = bf16[256,40,160]{2,1,0:T(8,128)(2,1)} async-done(((bf16[64,40,160]{2,1,0:T(8,128)(2,1)}), bf16[256,40,160]{2,1,0:T(8,128)(2,1)}) %all-gather.6.cloned.1.call-update) | async-done | bytes 3276816 | tf_op jit(solution)/shard_map/all_gather | solution.py:11
  145.1 4.9 %reduce_sum.62 = bf16[64,40,160]{2,1,0:T(8,128)(2,1)} reduce(bf16[4,64,40,160]{3,2,1,0:T(8,128)(2,1)} %bitcast.131, bf16[]{:T(256)} %constant.38.clone.1), dimensions={0}, to_apply=%region_2.0 | reduce | flops 1228800 | bytes 4096002 | tf_op jit(solution)/shard_map/reduce_sum | solution.py:11
  150.0 93.2 %all-gather.8.cloned.1.call-done = bf16[256,40,160]{2,1,0:T(8,128)(2,1)} async-done(((bf16[64,40,160]{2,1,0:T(8,128)(2,1)}), bf16[256,40,160]{2,1,0:T(8,128)(2,1)}) %all-gather.8.cloned.1.call-update) | async-done | bytes 3276816 | tf_op jit(solution)/shard_map/all_gather | solution.py:11
  243.2 4.9 %reduce_sum.63 = bf16[64,40,160]{2,1,0:T(8,128)(2,1)} reduce(bf16[4,64,40,160]{3,2,1,0:T(8,128)(2,1)} %bitcast.132, bf16[]{:T(256)} %constant.38.clone.1), dimensions={0}, to_apply=%region_3.0 | reduce | flops 1228800 | bytes 4096002 | tf_op jit(solution)/shard_map/reduce_sum | solution.py:11
  248.2 0.0 copy-done.4
  248.2 2.5 fusion.24
  250.7 2.7 %all-gather.2 = bf16[128,40,80]{2,1,0:T(8,128)(2,1)S(1)} all-gather(bf16[64,40,80]{2,1,0:T(8,128)(2,1)S(1)} %fusion.24), channel_id=4, replica_groups=mesh['ga'=2,'gx'=4,'gy'=2,'col'=2] {'col'}, dimensions={0}, use_global_device_ids=true | all-gather | bytes 1228800 | tf_op jit(solution)/shard_map/all_gather | solution.py:73
  253.5 0.3 convert_reduce_fusion
  253.8 0.5 fusion.3
  254.3 0.0 copy-done.8
  254.3 0.0 copy-done.9
  254.3 0.0 copy-start.5
  254.3 0.5 fusion.27
  254.8 0.2 copy-done.5
  255.0 1.2 fusion.47
  (12 shorter events, 0.1 us)
Async XLA Ops:
  7.2 4.4 %copy-start = (bf16[128,4,64]{0,2,1:T(8,128)(2,1)S(1)}, bf16[128,4,64]{0,2,1:T(8,128)(2,1)}, u32[]{:S(2)}) copy-start(bf16[128,4,64]{0,2,1:T(8,128)(2,1)} %param.15) | copy-start | bytes 196612
  7.2 3.2 %copy-start.2 = (bf16[1,40,80,128]{3,2,1,0:T(8,128)(2,1)S(1)}, bf16[1,40,80,128]{3,2,1,0:T(8,128)(2,1)}, u32[]{:S(2)}) copy-start(bf16[1,40,80,128]{3,2,1,0:T(8,128)(2,1)} %param.10) | copy-start | bytes 2457604
  7.2 4.4 %copy-start.6 = (f32[128]{0:T(128)S(1)}, f32[128]{0:T(128)}, u32[]{:S(2)}) copy-start(f32[128]{0:T(128)} %param.14) | copy-start | bytes 1540
  7.2 4.4 %copy-start.7 = (f32[128]{0:T(128)S(1)}, f32[128]{0:T(128)}, u32[]{:S(2)}) copy-start(f32[128]{0:T(128)} %param.13) | copy-start | bytes 1540
  7.2 137.9 %all-gather.6.cloned.1.call-start = ((), (), s32[]{:S(2)}) async-start(), calls=%async_computation | async-start | bytes 6553600 | tf_op jit(solution)/shard_map/all_gather | solution.py:11
  13.7 2.6 copy-start.1
  45.3 197.9 %all-gather.8.cloned.1.call-start = ((), (), s32[]{:S(2)}) async-start(), calls=%async_computation.1 | async-start | bytes 6553600 | tf_op jit(solution)/shard_map/all_gather | solution.py:11
  49.4 1.1 copy-start.3
  75.1 26.9 %copy-start.10 = (bf16[128,64]{0,1:T(8,128)(2,1)S(1)}, bf16[128,64]{0,1:T(8,128)(2,1)}, u32[]{:S(2)}) copy-start(bf16[128,64]{0,1:T(8,128)(2,1)} %param.16) | copy-start | bytes 49156
  243.2 4.9 %copy-start.4 = (bf16[64,40,160]{2,1,0:T(8,128)(2,1)S(1)}, bf16[64,40,160]{2,1,0:T(8,128)(2,1)}, u32[]{:S(2)}) copy-start(bf16[64,40,160]{2,1,0:T(8,128)(2,1)} %copy.52) | copy-start | bytes 2457604
  253.5 0.8 copy-start.8
  253.5 0.8 copy-start.9
  254.3 0.7 copy-start.5
Sparse Core Ops, SparseCore 0:
  45.4 99.6 all-gather.5
  146.7 96.4 all-gather.7
